TPU v7x, 32 devices: a whole 2x2x4 slice. The times are simulated.
32 devices in a mesh: gx: 4 (over y, core), gy: 4 (over z), gz: 2 (over x).
Axes of the slice: x: 2, y: 2, z: 4, core: 2. Of those that a mesh axis runs over, the one named last changes fastest.
Arguments:
- stream: bfloat16 [8192, 8192], P(('gx', 'gy', 'gz')), may hold values from -4 to 4
- segment_ids: int32 [8192], P(('gx', 'gy', 'gz')), may hold values from 0 to 8191, as said below
- positions: int32 [8192], P(('gx', 'gy', 'gz')), may hold values from 0 to 255, as said below
- norm_gain: bfloat16 [1, 8192], P(None, ('gx', 'gy', 'gz')), may hold values from 0.099609375 to 1.8984375
- q_weight: bfloat16 [1, 8192, 512], P(None, ('gx', 'gy', 'gz')), as said below
- k_weight: bfloat16 [1, 8192, 128], P(None, ('gx', 'gy', 'gz')), as said below
- v_weight: bfloat16 [1, 8192, 128], P(None, ('gx', 'gy', 'gz')), may hold values from -0.0625 to 0.0625
- o_weight: bfloat16 [1, 512, 8192], P(None, None, ('gx', 'gy', 'gz')), may hold values from -0.25 to 0.25
Outputs:
- result: bfloat16 [8192, 8192], P(('gx', 'gy', 'gz'))
Inputs may be any that keep to these rules, and one draw needn't show every extreme that they name: `segment_ids`: each token's id is the index of its document's first token, so ids never fall along the tokens; every document lies inside one aligned block of 256 tokens, every block starts a new document, and the last token is a document of its own. `positions`: counts from 0 at a document's first token and rises by one per token. `q_weight`: A projection scaled by its fan-in. `k_weight`: A projection scaled by its fan-in.
All inputs are finite; a program needn't handle non-finite values.
Results may differ from a plain program's by a relative error of at most 0.0064.
Values may be sent and summed in bfloat16 or wider, within the bound.
A program may use at most 128 MiB of HBM per device.

v0:
```python
import math
import jax
import jax.numpy as jnp
from jax import lax
from jax.sharding import PartitionSpec as P


def rotate(values, positions):
    width = values.shape[-1]
    half = width // 2
    freqs = jnp.exp(-math.log(500000.0) * jnp.arange(half, dtype=jnp.float32) * 2.0 / width)
    angles = positions.astype(jnp.float32)[:, None] * freqs[None, :]
    cosine = jnp.concatenate([jnp.cos(angles), jnp.cos(angles)], -1)[:, None, :]
    sine = jnp.concatenate([jnp.sin(angles), jnp.sin(angles)], -1)[:, None, :]
    turned = jnp.concatenate([-values[..., half:], values[..., :half]], -1)
    return values * cosine + turned * sine


def attend(queries, keys, values, segment_ids, positions):
    count = queries.shape[0]
    scores = jnp.einsum(
        "thd,sd->hts", queries, keys, preferred_element_type=jnp.float32
    ) / math.sqrt(keys.shape[-1])
    allowed = (segment_ids[:, None] == segment_ids[None, :]) & (
        positions[None, :] <= positions[:, None]
    )
    scores = jnp.where(allowed[None], scores, -1e30)
    peak = jnp.max(scores, -1, keepdims=True)
    expd = jnp.exp(scores - peak)
    probs = (expd / jnp.sum(expd, -1, keepdims=True)).astype(jnp.bfloat16)
    mixed = jnp.einsum("hts,sd->thd", probs, values, preferred_element_type=jnp.float32)
    return mixed.astype(jnp.bfloat16).reshape(count, -1)


def body(stream, segment_ids, positions, norm_gain, q_weight, k_weight, v_weight, o_weight):
    count = stream.shape[0]
    head_size = k_weight.shape[2]
    current = stream
    widened = lax.optimization_barrier(current).astype(jnp.float32)
    inverse = lax.rsqrt(jnp.mean(widened * widened, -1, keepdims=True) + 1e-05)
    scaled = widened * inverse
    inner = (
        lax.all_gather(norm_gain[0], "gz", axis=0, tiled=True),
        lax.all_gather(q_weight[0], "gz", axis=0, tiled=True),
        lax.all_gather(k_weight[0], "gz", axis=0, tiled=True),
        lax.all_gather(v_weight[0], "gz", axis=0, tiled=True),
    )
    middle = (
        lax.all_gather(inner[0], "gy", axis=0, tiled=True),
        lax.all_gather(inner[1], "gy", axis=0, tiled=True),
        lax.all_gather(inner[2], "gy", axis=0, tiled=True),
        lax.all_gather(inner[3], "gy", axis=0, tiled=True),
    )
    gain_piece = lax.all_gather(middle[0], "gx", axis=0, tiled=True)
    query_piece = lax.all_gather(middle[1], "gx", axis=0, tiled=True)
    key_piece = lax.all_gather(middle[2], "gx", axis=0, tiled=True)
    value_piece = lax.all_gather(middle[3], "gx", axis=0, tiled=True)
    normed = (scaled * gain_piece.astype(jnp.float32)[None, :]).astype(jnp.bfloat16)
    query_raw = jnp.dot(normed, query_piece, preferred_element_type=jnp.float32)
    key_raw = jnp.dot(normed, key_piece, preferred_element_type=jnp.float32)
    value_raw = jnp.dot(normed, value_piece, preferred_element_type=jnp.float32)
    queries = rotate(query_raw.reshape(count, -1, head_size), positions).astype(jnp.bfloat16)
    keys = rotate(key_raw[:, None, :], positions)[:, 0, :].astype(jnp.bfloat16)
    values = value_raw.astype(jnp.bfloat16)
    mixed = attend(queries, keys, values, segment_ids, positions)
    inner_cols = lax.all_gather(o_weight[0], "gz", axis=1, tiled=True)
    middle_cols = lax.all_gather(inner_cols, "gy", axis=1, tiled=True)
    branch = jnp.dot(
        mixed,
        lax.all_gather(middle_cols, "gx", axis=1, tiled=True),
        preferred_element_type=jnp.float32,
    )
    current = (widened + branch).astype(jnp.bfloat16)
    return current


def solution(mesh):
    in_specs = (
        P(("gx", "gy", "gz"), None),
        P(("gx", "gy", "gz")),
        P(("gx", "gy", "gz")),
        P(None, ("gx", "gy", "gz")),
        P(None, ("gx", "gy", "gz"), None),
        P(None, ("gx", "gy", "gz"), None),
        P(None, ("gx", "gy", "gz"), None),
        P(None, None, ("gx", "gy", "gz")),
    )
    out_specs = P(("gx", "gy", "gz"), None)
    return jax.shard_map(body, mesh=mesh, in_specs=in_specs, out_specs=out_specs, check_vma=False)
```

profile of v0, /device:TPU:0, one launch (start us, length us, event | category | flops | bytes accessed | tf_op | source)
XLA Modules:
  0.0 307.4 jit_solution(744721059821343803)
XLA Ops:
  6.5 0.0 copy-start
  6.5 0.0 all-gather.26.cloned.1.call-start
  6.5 12.0 %all-gather.9 = bf16[1,512,512]{2,1,0:T(8,128)(2,1)} all-gather(bf16[1,256,512]{2,1,0:T(8,128)(2,1)} %param.12), channel_id=11, replica_groups=mesh['gx'=4,'gy'=4,'gz'=2] {'gz'}, dimensions={1}, use_global_device_ids=true | all-gather | bytes 786432 | tf_op jit(solution)/shard_map/all_gather | solution.py:44
  18.6 0.0 all-gather.26.cloned.1.call-update
  18.6 0.0 copy-start.3
  18.6 0.0 copy-start.1
  18.6 0.0 all-gather.30.cloned.1.call-start
  18.7 8.5 %all-gather.12 = bf16[1,512,512]{2,1,0:T(8,128)(2,1)} all-gather(bf16[1,512,256]{2,1,0:T(8,128)(2,1)} %param.15), channel_id=14, replica_groups=mesh['gx'=4,'gy'=4,'gz'=2] {'gz'}, dimensions={2}, use_global_device_ids=true | all-gather | bytes 786432 | tf_op jit(solution)/shard_map/all_gather | solution.py:66
  27.1 0.0 all-gather.30.cloned.1.call-update
  27.2 0.0 all-gather.24.cloned.1.call-start
  27.2 5.2 %all-gather.6 = bf16[1,512,128]{2,1,0:T(8,128)(2,1)S(1)} all-gather(bf16[1,256,128]{2,1,0:T(8,128)(2,1)} %param.13), channel_id=8, replica_groups=mesh['gx'=4,'gy'=4,'gz'=2] {'gz'}, dimensions={1}, use_global_device_ids=true | all-gather | bytes 196608 | tf_op jit(solution)/shard_map/all_gather | solution.py:45
  32.4 23.9 %all-gather.7 = bf16[1,2048,128]{2,1,0:T(8,128)(2,1)} all-gather(bf16[1,512,128]{2,1,0:T(8,128)(2,1)S(1)} %all-gather.6), channel_id=9, replica_groups=mesh['gx'=4,'gy'=4,'gz'=2] {'gy'}, dimensions={1}, use_global_device_ids=true | all-gather | bytes 655360 | tf_op jit(solution)/shard_map/all_gather | solution.py:51
  56.2 0.0 all-gather.24.cloned.1.call-update
  56.2 0.0 all-gather.28.cloned.1.call-start
  56.3 16.9 %all-gather.26.cloned.1.call-done = bf16[1,2048,512]{2,1,0:T(8,128)(2,1)} async-done(((bf16[1,512,512]{2,1,0:T(8,128)(2,1)}), bf16[1,2048,512]{2,1,0:T(8,128)(2,1)}) %all-gather.26.cloned.1.call-update) | async-done | bytes 2097168 | tf_op jit(solution)/shard_map/all_gather | solution.py:50
  73.2 0.0 all-gather.28.cloned.1.call-update
  73.2 0.0 copy-start.2
  73.2 0.0 all-gather.22.cloned.1.call-start
  73.2 0.0 copy-done
  73.3 4.9 %all-gather.3 = bf16[1,512,128]{2,1,0:T(8,128)(2,1)S(1)} all-gather(bf16[1,256,128]{2,1,0:T(8,128)(2,1)S(1)} %copy-done), channel_id=5, replica_groups=mesh['gx'=4,'gy'=4,'gz'=2] {'gz'}, dimensions={1}, use_global_device_ids=true | all-gather | bytes 196608 | tf_op jit(solution)/shard_map/all_gather | solution.py:46
  78.2 20.2 %all-gather.4 = bf16[1,2048,128]{2,1,0:T(8,128)(2,1)} all-gather(bf16[1,512,128]{2,1,0:T(8,128)(2,1)S(1)} %all-gather.3), channel_id=6, replica_groups=mesh['gx'=4,'gy'=4,'gz'=2] {'gy'}, dimensions={1}, use_global_device_ids=true | all-gather | bytes 655360 | tf_op jit(solution)/shard_map/all_gather | solution.py:52
  98.4 0.0 all-gather.22.cloned.1.call-update
  98.4 0.0 all-gather.32.cloned.1.call-start
  98.4 26.2 %all-gather.30.cloned.1.call-done = bf16[1,512,2048]{2,1,0:T(8,128)(2,1)} async-done(((bf16[1,512,512]{2,1,0:T(8,128)(2,1)}), bf16[1,512,2048]{2,1,0:T(8,128)(2,1)}) %all-gather.30.cloned.1.call-update) | async-done | bytes 2097168 | tf_op jit(solution)/shard_map/all_gather | solution.py:67
  124.7 0.0 all-gather.32.cloned.1.call-update
  124.7 0.0 copy-done.3
  124.7 4.2 %all-gather = bf16[1,512]{1,0:T(2,128)(2,1)S(1)} all-gather(bf16[1,256]{1,0:T(2,128)(2,1)S(1)} %copy-done.3), channel_id=2, replica_groups=mesh['gx'=4,'gy'=4,'gz'=2] {'gz'}, dimensions={1}, use_global_device_ids=true | all-gather | bytes 1536 | tf_op jit(solution)/shard_map/all_gather | solution.py:43
  128.9 11.9 %all-gather.1 = bf16[1,2048]{1,0:T(2,128)(2,1)S(1)} all-gather(bf16[1,512]{1,0:T(2,128)(2,1)S(1)} %all-gather), channel_id=3, replica_groups=mesh['gx'=4,'gy'=4,'gz'=2] {'gy'}, dimensions={1}, use_global_device_ids=true | all-gather | bytes 5120 | tf_op jit(solution)/shard_map/all_gather | solution.py:49
  140.9 5.5 %all-gather.2 = bf16[1,8192]{1,0:T(2,128)(2,1)S(1)} all-gather(bf16[1,2048]{1,0:T(2,128)(2,1)S(1)} %all-gather.1), channel_id=4, replica_groups=mesh['gx'=4,'gy'=4,'gz'=2] {'gx'}, dimensions={1}, use_global_device_ids=true | all-gather | bytes 20480 | tf_op jit(solution)/shard_map/all_gather | solution.py:54
  146.4 0.0 copy-done.1
  146.4 3.1 %fusion.2 = f32[256]{0:T(256)S(1)} fusion(bf16[256,8192]{1,0:T(8,128)(2,1)} %param.8), kind=kLoop, calls=%fused_computation.5 | loop fusion | flops 6291200 | bytes 4195328 | tf_op jit(solution)/shard_map/reduce_sum | solution.py:40
  149.6 0.0 copy-done.2
  149.6 0.1 compare_and_fusion
  149.7 0.3 multiply_cosine_fusion
  150.0 0.0 all-gather.24.cloned.1.call-done
  150.1 4.6 %fusion.8 = f32[256,128]{0,1:T(8,128)S(1)} fusion(bf16[1,8192,128]{2,1,0:T(8,128)(2,1)} %all-gather.24.cloned.1.call-done, bf16[256,8192]{1,0:T(8,128)(2,1)} %param.8, f32[8192]{0:T(1024)S(1)} %bitcast.83, f32[256]{0:T(256)S(1)} %add_rsqrt_fusion), kind=kOutput, calls=%fused_computation.11 | convolution fusion | flops 545259520 | bytes 6456320 | tf_op jit(solution)/shard_map/dot_general | solution.py:60
  154.7 0.1 copy.10
  154.8 0.1 copy.9
  154.9 52.9 %all-gather.28.cloned.1.call-done = bf16[1,8192,512]{2,1,0:T(8,128)(2,1)} async-done(((bf16[1,2048,512]{2,1,0:T(8,128)(2,1)}), bf16[1,8192,512]{2,1,0:T(8,128)(2,1)}) %all-gather.28.cloned.1.call-update) | async-done | bytes 8388624 | tf_op jit(solution)/shard_map/all_gather | solution.py:55
  207.9 7.0 %fusion.6 = f32[256,512]{1,0:T(8,128)S(1)} fusion(bf16[1,8192,512]{2,1,0:T(8,128)(2,1)} %all-gather.28.cloned.1.call-done, bf16[256,8192]{1,0:T(8,128)(2,1)} %param.8, f32[8192]{0:T(1024)S(1)} %bitcast.84, f32[256]{0:T(256)S(1)} %add_rsqrt_fusion), kind=kOutput, calls=%fused_computation.9 | convolution fusion | flops 2155872256 | bytes 13140992 | tf_op jit(solution)/shard_map/dot_general | solution.py:59
  214.9 0.2 reshape.93
  215.1 0.3 slice_negate_fusion
  215.4 0.4 maximum_multiply_fusion
  215.8 0.1 mul.85
  215.9 0.5 fusion.44
  216.4 15.4 %all-gather.22.cloned.1.call-done = bf16[1,8192,128]{2,1,0:T(8,128)(2,1)} async-done(((bf16[1,2048,128]{2,1,0:T(8,128)(2,1)}), bf16[1,8192,128]{2,1,0:T(8,128)(2,1)}) %all-gather.22.cloned.1.call-update) | async-done | bytes 2097168 | tf_op jit(solution)/shard_map/all_gather | solution.py:57
  231.9 4.7 %convolution_convert_fusion = bf16[128,4,256]{2,0,1:T(8,128)(2,1)S(1)} fusion(bf16[1,8192,128]{2,1,0:T(8,128)(2,1)} %all-gather.22.cloned.1.call-done, f32[4,256,256]{1,2,0:T(8,128)S(1)} %get-tuple-element.15, f32[4,256]{1,0:T(4,128)S(1)} %get-tuple-element.14, bf16[256,8192]{1,0:T(8,128)(2,1)} %param.8, f32[8192]{0:T(1024)S(1)} %bitcast.85, ...), kind=kOutput, calls=%fused_computation.20 | convolution fusion | flops 613056512 | bytes 7640064 | tf_op jit(solution)/shard_map/hts,sd->thd/dot_general | solution.py:31
  236.5 55.0 %all-gather.32.cloned.1.call-done = bf16[1,512,8192]{2,1,0:T(8,128)(2,1)} async-done(((bf16[1,512,2048]{2,1,0:T(8,128)(2,1)}), bf16[1,512,8192]{2,1,0:T(8,128)(2,1)}) %all-gather.32.cloned.1.call-update) | async-done | bytes 8388624 | tf_op jit(solution)/shard_map/all_gather | solution.py:70
  291.6 9.0 %fusion.1 = bf16[256,8192]{1,0:T(8,128)(2,1)} fusion(bf16[256,512]{0,1:T(8,128)(2,1)S(1)} %bitcast.82, bf16[256,8192]{1,0:T(8,128)(2,1)} %param.8, bf16[1,512,8192]{2,1,0:T(8,128)(2,1)} %all-gather.32.cloned.1.call-done), kind=kOutput, calls=%fused_computation.4 | convolution fusion | flops 2153775104 | bytes 17039360 | tf_op jit(solution)/shard_map/dot_general | solution.py:68
  (6 shorter events, 0.1 us)
Async XLA Ops:
  6.5 66.7 %copy-start = (bf16[1,256,128]{2,1,0:T(8,128)(2,1)S(1)}, bf16[1,256,128]{2,1,0:T(8,128)(2,1)}, u32[]{:S(2)}) copy-start(bf16[1,256,128]{2,1,0:T(8,128)(2,1)} %param.14) | copy-start | bytes 196612
  6.5 66.6 %all-gather.26.cloned.1.call-start = ((), (), s32[]{:S(2)}) async-start(), calls=%async_computation.2 | async-start | bytes 2621440 | tf_op jit(solution)/shard_map/all_gather | solution.py:50
  18.6 106.1 %copy-start.3 = (bf16[1,256]{1,0:T(2,128)(2,1)S(1)}, bf16[1,256]{1,0:T(2,128)(2,1)}, u32[]{:S(2)}) copy-start(bf16[1,256]{1,0:T(2,128)(2,1)} %param.11) | copy-start | bytes 1540
  18.6 127.8 %copy-start.1 = (s32[256]{0:T(256)S(1)}, s32[256]{0:T(256)}, u32[]{:S(2)}) copy-start(s32[256]{0:T(256)} %param.10) | copy-start | bytes 3076
  18.6 106.0 %all-gather.30.cloned.1.call-start = ((), (), s32[]{:S(2)}) async-start(), calls=%async_computation.4 | async-start | bytes 2621440 | tf_op jit(solution)/shard_map/all_gather | solution.py:67
  27.2 122.9 %all-gather.24.cloned.1.call-start = ((), (), s32[]{:S(2)}) async-start(), calls=%async_computation.1 | async-start | bytes 2621440 | tf_op jit(solution)/shard_map/all_gather | solution.py:56
  56.2 151.6 %all-gather.28.cloned.1.call-start = ((), (), s32[]{:S(2)}) async-start(), calls=%async_computation.3 | async-start | bytes 10485760 | tf_op jit(solution)/shard_map/all_gather | solution.py:55
  73.2 76.4 %copy-start.2 = (s32[256]{0:T(256)S(1)}, s32[256]{0:T(256)}, u32[]{:S(2)}) copy-start(s32[256]{0:T(256)} %param.9) | copy-start | bytes 3076
  73.2 158.7 %all-gather.22.cloned.1.call-start = ((), (), s32[]{:S(2)}) async-start(), calls=%async_computation | async-start | bytes 2621440 | tf_op jit(solution)/shard_map/all_gather | solution.py:57
  98.4 193.2 %all-gather.32.cloned.1.call-start = ((), (), s32[]{:S(2)}) async-start(), calls=%async_computation.5 | async-start | bytes 10485760 | tf_op jit(solution)/shard_map/all_gather | solution.py:70
Sparse Core Ops, SparseCore 0:
  18.7 54.3 all-gather.25
  74.7 49.8 all-gather.29
  126.2 21.8 all-gather.23
  149.6 58.2 all-gather.27
  209.3 22.5 all-gather.21
  233.3 58.2 all-gather.31
where the time goes:
time: 308 us; the launch traced here: 307 us
  waiting for transfers between devices  167 us (54%)
  blocking collectives  96.3 us (31%)
  matrix products  25.9 us (8%)
  between operations  13.6 us (4%)
  other arithmetic  4.37 us (1%)
    all_gather x1, waiting for transfers between devices, body(): lax.all_gather(middle_cols, 'gx', axis=1, tiled=True)  55 us
    all_gather x1, waiting for transfers between devices, body(): query_piece = lax.all_gather(middle[1], 'gx', axis=0, tiled=True)  52.9 us
    all_gather x1, waiting for transfers between devices, body(): middle_cols = lax.all_gather(inner_cols, 'gy', axis=1, tiled=True)  26.2 us
    all_gather x1, blocking collectives, body(): lax.all_gather(inner[2], 'gy', axis=0, tiled=True)  23.9 us
    all_gather x1, blocking collectives, body(): lax.all_gather(inner[3], 'gy', axis=0, tiled=True)  20.2 us
    all_gather x1, waiting for transfers between devices, body(): lax.all_gather(inner[1], 'gy', axis=0, tiled=True)  16.9 us
    all_gather x1, waiting for transfers between devices, body(): value_piece = lax.all_gather(middle[3], 'gx', axis=0, tiled=True)  15.4 us
    all_gather x1, blocking collectives, body(): lax.all_gather(q_weight[0], 'gz', axis=0, tiled=True)  12 us
  transfers between devices with their start and end apart: 6, of which 5 were waited for; matrix products, arithmetic and copies ran while one was open for 7% of the time, Pallas kernels for 0%

commit v1 on v0

--- a/solution.py
+++ b/solution.py
@@ -52,7 +52,12 @@
         lax.all_gather(inner[3], "gy", axis=0, tiled=True),
     )
     gain_piece = lax.all_gather(middle[0], "gx", axis=0, tiled=True)
-    query_piece = lax.all_gather(middle[1], "gx", axis=0, tiled=True)
+    ring = [middle[1]]
+    for hop in range(3):
+        ring.append(lax.ppermute(ring[-1], "gx", [(dev, (dev + 1) % 4) for dev in range(4)]))
+    query_piece = jnp.roll(
+        jnp.concatenate(ring[::-1], axis=0), (lax.axis_index("gx") + 1) * ring[0].shape[0], axis=0
+    )
     key_piece = lax.all_gather(middle[2], "gx", axis=0, tiled=True)
     value_piece = lax.all_gather(middle[3], "gx", axis=0, tiled=True)
     normed = (scaled * gain_piece.astype(jnp.float32)[None, :]).astype(jnp.bfloat16)

time: 308 us -> 301 us (0.977)
  waiting for transfers between devices: 167 us -> 134 us
  blocking collectives: 96.3 us -> 118 us
  local copies, waits for them, and re-layouts: 0.48 us -> 8.09 us
  matrix products: 25.9 us -> 21.2 us
    ppermute x0 -> x3, waiting for transfers between devices: none -> 89.7 us  [body(): lax.ppermute(ring[-1], 'gx', [(dev, (dev + 1) % 4) for dev in range(4)])]
    all_gather x1, waiting for transfers between devices: 55 us -> 0.02 us  [body(): lax.all_gather(middle_cols, 'gx', axis=1, tiled=True)]
    all_gather x1 -> x0, waiting for transfers between devices: 52.9 us -> none  [body(): query_piece = lax.all_gather(middle[1], 'gx', axis=0, tiled=True)]
    all_gather x1, waiting for transfers between devices: 16.9 us -> 43.6 us  [body(): lax.all_gather(inner[1], 'gy', axis=0, tiled=True)]
    all_gather x1, waiting for transfers between devices: 26.2 us -> 0.02 us  [body(): middle_cols = lax.all_gather(inner_cols, 'gy', axis=1, tiled=True)]
    all_gather x1, blocking collectives: 5.47 us -> 25.7 us  [body(): gain_piece = lax.all_gather(middle[0], 'gx', axis=0, tiled=True)]
    all_gather x1, waiting for transfers between devices: 15.4 us -> 0.02 us  [body(): value_piece = lax.all_gather(middle[3], 'gx', axis=0, tiled=True)]
    unnamed x8 -> x19, local copies, waits for them, and re-layouts: 0.02 us -> 7.5 us
  transfers between devices with their start and end apart: 6 -> 8, of which waited for: 5 -> 3; matrix products, arithmetic and copies ran while one was open for 7% -> 8% of each run, Pallas kernels for 0% -> 0%
where the time goes in v1:
time: 301 us; the launch traced here: 300 us
  waiting for transfers between devices  134 us (45%)
  blocking collectives  118 us (39%)
  matrix products  21.2 us (7%)
  between operations  13.4 us (4%)
  local copies, waits for them, and re-layouts  8.09 us (3%)
  other arithmetic  5.1 us (2%)
    ppermute x3, waiting for transfers between devices, body(): lax.ppermute(ring[-1], 'gx', [(dev, (dev + 1) % 4) for dev in range(4)])  89.7 us
    all_gather x1, waiting for transfers between devices, body(): lax.all_gather(inner[1], 'gy', axis=0, tiled=True)  43.6 us
    all_gather x1, blocking collectives, body(): gain_piece = lax.all_gather(middle[0], 'gx', axis=0, tiled=True)  25.7 us
    all_gather x1, blocking collectives, body(): lax.all_gather(inner[2], 'gy', axis=0, tiled=True)  23.9 us
    all_gather x1, blocking collectives, body(): lax.all_gather(inner[3], 'gy', axis=0, tiled=True)  21.3 us
    all_gather x1, blocking collectives, body(): inner_cols = lax.all_gather(o_weight[0], 'gz', axis=1, tiled=True)  12 us
    all_gather x1, blocking collectives, body(): lax.all_gather(inner[0], 'gy', axis=0, tiled=True)  11.9 us
    dot_general x1, matrix products, body(): jnp.dot(mixed, lax.all_gather(middle_cols, 'gx', axis=1, tiled=True), pre...  9.02 us
  transfers between devices with their start and end apart: 8, of which 3 were waited for; matrix products, arithmetic and copies ran while one was open for 8% of the time, Pallas kernels for 0%

profile of v1, /device:TPU:0, one launch (start us, length us, event | category | flops | bytes accessed | tf_op | source)
XLA Modules:
  0.0 300.1 jit_solution(5459810443050345550)
XLA Ops:
  6.5 0.0 copy-start.4
  6.5 0.0 copy-start.5
  6.5 0.0 all-gather.26.cloned.1.call-start
  6.5 12.0 %all-gather.11 = bf16[1,512,512]{2,1,0:T(8,128)(2,1)} all-gather(bf16[1,512,256]{2,1,0:T(8,128)(2,1)} %param.15), channel_id=13, replica_groups=mesh['gx'=4,'gy'=4,'gz'=2] {'gz'}, dimensions={2}, use_global_device_ids=true | all-gather | bytes 786432 | tf_op jit(solution)/shard_map/all_gather | solution.py:71
  18.6 0.0 all-gather.26.cloned.1.call-update
  18.6 0.0 all-gather.24.cloned.1.call-start
  18.6 8.5 %all-gather.9 = bf16[1,512,512]{2,1,0:T(8,128)(2,1)} all-gather(bf16[1,256,512]{2,1,0:T(8,128)(2,1)} %param.12), channel_id=11, replica_groups=mesh['gx'=4,'gy'=4,'gz'=2] {'gz'}, dimensions={1}, use_global_device_ids=true | all-gather | bytes 786432 | tf_op jit(solution)/shard_map/all_gather | solution.py:44
  27.1 0.0 all-gather.24.cloned.1.call-update
  27.1 0.0 all-gather.22.cloned.1.call-start
  27.2 5.1 %all-gather.6 = bf16[1,512,128]{2,1,0:T(8,128)(2,1)S(1)} all-gather(bf16[1,256,128]{2,1,0:T(8,128)(2,1)} %param.13), channel_id=8, replica_groups=mesh['gx'=4,'gy'=4,'gz'=2] {'gz'}, dimensions={1}, use_global_device_ids=true | all-gather | bytes 196608 | tf_op jit(solution)/shard_map/all_gather | solution.py:45
  32.3 23.9 %all-gather.7 = bf16[1,2048,128]{2,1,0:T(8,128)(2,1)} all-gather(bf16[1,512,128]{2,1,0:T(8,128)(2,1)S(1)} %all-gather.6), channel_id=9, replica_groups=mesh['gx'=4,'gy'=4,'gz'=2] {'gy'}, dimensions={1}, use_global_device_ids=true | all-gather | bytes 655360 | tf_op jit(solution)/shard_map/all_gather | solution.py:51
  56.2 0.0 all-gather.22.cloned.1.call-update
  56.2 0.0 all-gather.20.cloned.1.call-start
  56.3 5.1 %all-gather.3 = bf16[1,512,128]{2,1,0:T(8,128)(2,1)S(1)} all-gather(bf16[1,256,128]{2,1,0:T(8,128)(2,1)} %param.14), channel_id=5, replica_groups=mesh['gx'=4,'gy'=4,'gz'=2] {'gz'}, dimensions={1}, use_global_device_ids=true | all-gather | bytes 196608 | tf_op jit(solution)/shard_map/all_gather | solution.py:46
  61.4 21.3 %all-gather.4 = bf16[1,2048,128]{2,1,0:T(8,128)(2,1)} all-gather(bf16[1,512,128]{2,1,0:T(8,128)(2,1)S(1)} %all-gather.3), channel_id=6, replica_groups=mesh['gx'=4,'gy'=4,'gz'=2] {'gy'}, dimensions={1}, use_global_device_ids=true | all-gather | bytes 655360 | tf_op jit(solution)/shard_map/all_gather | solution.py:52
  82.8 0.0 all-gather.20.cloned.1.call-update
  82.8 0.0 all-gather.28.cloned.1.call-start
  82.8 0.0 all-gather.26.cloned.1.call-done
  82.9 0.5 all-gather.28.cloned.1.call-update
  83.4 43.6 %all-gather.24.cloned.1.call-done = bf16[1,2048,512]{2,1,0:T(8,128)(2,1)} async-done(((bf16[1,512,512]{2,1,0:T(8,128)(2,1)}), bf16[1,2048,512]{2,1,0:T(8,128)(2,1)}) %all-gather.24.cloned.1.call-update) | async-done | bytes 2097168 | tf_op jit(solution)/shard_map/all_gather | solution.py:50
  126.9 0.0 collective-permute-start
  126.9 36.9 %collective-permute-done = bf16[2048,512]{1,0:T(8,128)(2,1)S(1)} collective-permute-done((bf16[2048,512]{1,0:T(8,128)(2,1)}, bf16[2048,512]{1,0:T(8,128)(2,1)S(1)}, u32[]{:S(2)}, u32[]{:S(2)}) %collective-permute-start) | collective-permute-done | bytes 2097184 | tf_op jit(solution)/shard_map/ppermute | solution.py:57
  163.8 0.0 collective-permute-start.1
  163.9 4.4 %all-gather = bf16[1,512]{1,0:T(2,128)(2,1)S(1)} all-gather(bf16[1,256]{1,0:T(2,128)(2,1)} %param.11), channel_id=2, replica_groups=mesh['gx'=4,'gy'=4,'gz'=2] {'gz'}, dimensions={1}, use_global_device_ids=true | all-gather | bytes 1536 | tf_op jit(solution)/shard_map/all_gather | solution.py:43
  168.3 11.9 %all-gather.1 = bf16[1,2048]{1,0:T(2,128)(2,1)S(1)} all-gather(bf16[1,512]{1,0:T(2,128)(2,1)S(1)} %all-gather), channel_id=3, replica_groups=mesh['gx'=4,'gy'=4,'gz'=2] {'gy'}, dimensions={1}, use_global_device_ids=true | all-gather | bytes 5120 | tf_op jit(solution)/shard_map/all_gather | solution.py:49
  180.2 25.7 %all-gather.2 = bf16[1,8192]{1,0:T(2,128)(2,1)S(1)} all-gather(bf16[1,2048]{1,0:T(2,128)(2,1)S(1)} %all-gather.1), channel_id=4, replica_groups=mesh['gx'=4,'gy'=4,'gz'=2] {'gx'}, dimensions={1}, use_global_device_ids=true | all-gather | bytes 20480 | tf_op jit(solution)/shard_map/all_gather | solution.py:54
  206.0 0.7 convert_element_type.43
  206.7 0.0 collective-permute-done.1
  206.7 0.2 collective-permute-start.2
  206.9 3.2 %fusion.2 = f32[256]{0:T(256)S(1)} fusion(bf16[256,8192]{1,0:T(8,128)(2,1)} %param.8), kind=kLoop, calls=%fused_computation.5 | loop fusion | flops 6291200 | bytes 4195328 | tf_op jit(solution)/shard_map/reduce_sum | solution.py:40
  210.1 0.0 copy-done.4
  210.1 0.0 copy-done.5
  210.1 0.1 compare_and_fusion
  210.2 0.3 multiply_cosine_fusion
  210.5 0.0 all-gather.22.cloned.1.call-done
  210.6 0.0 copy-done.2
  210.6 4.6 %fusion.8 = f32[256,128]{0,1:T(8,128)S(1)} fusion(bf16[1,8192,128]{2,1,0:T(8,128)(2,1)} %all-gather.22.cloned.1.call-done, bf16[256,8192]{1,0:T(8,128)(2,1)} %param.8, f32[8192]{0:T(1024)S(1)} %bitcast.84, f32[256]{0:T(256)S(1)} %add_rsqrt_fusion), kind=kOutput, calls=%fused_computation.11 | convolution fusion | flops 545259520 | bytes 6456320 | tf_op jit(solution)/shard_map/dot_general | solution.py:65
  215.2 0.0 copy-start.1
  215.3 0.1 copy.10
  215.4 0.1 copy.9
  215.5 0.0 copy-start.3
  215.5 52.8 %collective-permute-done.2 = bf16[2048,512]{1,0:T(8,128)(2,1)} collective-permute-done((bf16[2048,512]{1,0:T(8,128)(2,1)}, bf16[2048,512]{1,0:T(8,128)(2,1)}, u32[]{:S(2)}, u32[]{:S(2)}) %collective-permute-start.2) | collective-permute-done | bytes 2097184 | tf_op jit(solution)/shard_map/ppermute | solution.py:57
  268.2 1.7 constant_dynamic-update-slice_fusion.7
  270.0 1.7 constant_dynamic-update-slice_fusion.6
  271.7 0.0 copy-done.3
  271.7 0.1 constant_dynamic-update-slice_fusion.5
  271.9 0.0 copy-done.1
  271.9 0.1 constant_dynamic-update-slice_fusion.4
  272.0 0.0 copy-start
  272.0 1.9 constant_dynamic-update-slice_fusion.3
  273.9 1.7 constant_dynamic-update-slice_fusion.2
  275.6 0.1 constant_dynamic-update-slice_fusion.1
  275.8 0.1 constant_dynamic-update-slice_fusion
  275.9 0.0 copy-done
  275.9 2.4 fusion.6
  278.3 0.2 reshape.93
  278.5 0.3 slice_negate_fusion
  278.8 0.4 maximum_multiply_fusion
  279.2 0.1 mul.89
  279.3 0.5 fusion.45
  279.8 0.0 all-gather.20.cloned.1.call-done
  279.9 4.7 %convolution_convert_fusion = bf16[128,4,256]{2,0,1:T(8,128)(2,1)S(1)} fusion(bf16[1,8192,128]{2,1,0:T(8,128)(2,1)} %all-gather.20.cloned.1.call-done, f32[4,256,256]{1,2,0:T(8,128)S(1)} %get-tuple-element.15, f32[4,256]{1,0:T(4,128)S(1)} %get-tuple-element.14, bf16[256,8192]{1,0:T(8,128)(2,1)} %param.8, f32[8192]{0:T(1024)S(1)} %bitcast.86, ...), kind=kOutput, calls=%fused_computation.20 | convolution fusion | flops 613056512 | bytes 7640064 | tf_op jit(solution)/shard_map/hts,sd->thd/dot_general | solution.py:31
  284.5 0.0 all-gather.28.cloned.1.call-done
  284.6 9.0 %fusion.1 = bf16[256,8192]{1,0:T(8,128)(2,1)} fusion(bf16[256,512]{0,1:T(8,128)(2,1)S(1)} %bitcast.83, bf16[256,8192]{1,0:T(8,128)(2,1)} %param.8, bf16[1,512,8192]{2,1,0:T(8,128)(2,1)} %all-gather.28.cloned.1.call-done), kind=kOutput, calls=%fused_computation.4 | convolution fusion | flops 2153775104 | bytes 17039360 | tf_op jit(solution)/shard_map/dot_general | solution.py:73
  (6 shorter events, 0.1 us)
Async XLA Ops:
  6.5 203.5 %copy-start.4 = (s32[256]{0:T(256)S(1)}, s32[256]{0:T(256)}, u32[]{:S(2)}) copy-start(s32[256]{0:T(256)} %param.10) | copy-start | bytes 3076
  6.5 203.5 %copy-start.5 = (s32[256]{0:T(256)S(1)}, s32[256]{0:T(256)}, u32[]{:S(2)}) copy-start(s32[256]{0:T(256)} %param.9) | copy-start | bytes 3076
  6.5 76.3 %all-gather.26.cloned.1.call-start = ((), (), s32[]{:S(2)}) async-start(), calls=%async_computation.3 | async-start | bytes 2621440 | tf_op jit(solution)/shard_map/all_gather | solution.py:72
  18.6 108.4 %all-gather.24.cloned.1.call-start = ((), (), s32[]{:S(2)}) async-start(), calls=%async_computation.2 | async-start | bytes 2621440 | tf_op jit(solution)/shard_map/all_gather | solution.py:50
  27.1 183.4 %all-gather.22.cloned.1.call-start = ((), (), s32[]{:S(2)}) async-start(), calls=%async_computation.1 | async-start | bytes 2621440 | tf_op jit(solution)/shard_map/all_gather | solution.py:61
  56.2 223.6 %all-gather.20.cloned.1.call-start = ((), (), s32[]{:S(2)}) async-start(), calls=%async_computation | async-start | bytes 2621440 | tf_op jit(solution)/shard_map/all_gather | solution.py:62
  82.8 201.8 %all-gather.28.cloned.1.call-start = ((), (), s32[]{:S(2)}) async-start(), calls=%async_computation.4 | async-start | bytes 10485760 | tf_op jit(solution)/shard_map/all_gather | solution.py:75
  126.9 36.9 %collective-permute-start = (bf16[2048,512]{1,0:T(8,128)(2,1)}, bf16[2048,512]{1,0:T(8,128)(2,1)S(1)}, u32[]{:S(2)}, u32[]{:S(2)}) collective-permute-start(bf16[2048,512]{1,0:T(8,128)(2,1)} %bitcast.79), channel_id=1, source_target_pairs={{0,8},{8,16},{16,24},{24,0},{1,9},{9,17},{17,25},{25,1},{2,10},{10... | collective-permute-start | bytes 6291464 | tf_op jit(solution)/shard_map/ppermute | solution.py:57
  163.8 46.7 %copy-start.2 = (bf16[2048,512]{1,0:T(8,128)(2,1)}, bf16[2048,512]{1,0:T(8,128)(2,1)S(1)}, u32[]{:S(2)}) copy-start(bf16[2048,512]{1,0:T(8,128)(2,1)S(1)} %collective-permute-done) | copy-start | bytes 6291460
  163.8 42.8 %collective-permute-start.1 = (bf16[2048,512]{1,0:T(8,128)(2,1)S(1)}, bf16[2048,512]{1,0:T(8,128)(2,1)}, u32[]{:S(2)}, u32[]{:S(2)}) collective-permute-start(bf16[2048,512]{1,0:T(8,128)(2,1)S(1)} %collective-permute-done), channel_id=1, source_target_pairs={{0,8},{8,16},{16,24},{24,0},{1,9},{9,17},{17,25},{25,1},{2,10},{10... | collective-permute-start | bytes 6291464 | tf_op jit(solution)/shard_map/ppermute | solution.py:57
  206.7 61.5 %collective-permute-start.2 = (bf16[2048,512]{1,0:T(8,128)(2,1)}, bf16[2048,512]{1,0:T(8,128)(2,1)}, u32[]{:S(2)}, u32[]{:S(2)}) collective-permute-start(bf16[2048,512]{1,0:T(8,128)(2,1)} %collective-permute-done.1), channel_id=1, source_target_pairs={{0,8},{8,16},{16,24},{24,0},{1,9},{9,17},{17,25},{25,1},{2,10},{10... | collective-permute-start | bytes 6291464 | tf_op jit(solution)/shard_map/ppermute | solution.py:57
  215.2 56.6 %copy-start.1 = (bf16[1,2048,512]{2,1,0:T(8,128)(2,1)S(1)}, bf16[1,2048,512]{2,1,0:T(8,128)(2,1)}, u32[]{:S(2)}) copy-start(bf16[1,2048,512]{2,1,0:T(8,128)(2,1)} %all-gather.24.cloned.1.call-done) | copy-start | bytes 6291460
  215.5 56.2 %copy-start.3 = (bf16[2048,512]{1,0:T(8,128)(2,1)S(1)}, bf16[2048,512]{1,0:T(8,128)(2,1)}, u32[]{:S(2)}) copy-start(bf16[2048,512]{1,0:T(8,128)(2,1)} %copy-done.2) | copy-start | bytes 6291460
  272.0 3.9 %copy-start = (bf16[256,8192]{1,0:T(8,128)(2,1)S(1)}, bf16[256,8192]{1,0:T(8,128)(2,1)}, u32[]{:S(2)}) copy-start(bf16[256,8192]{1,0:T(8,128)(2,1)} %param.8) | copy-start | bytes 12582916
Sparse Core Ops, SparseCore 0:
  18.7 62.2 all-gather.25
  82.6 44.2 all-gather.23
  128.5 27.0 all-gather.21
  157.1 28.2 all-gather.19
  186.8 78.4 all-gather.27
